TPU v7x, 32 devices: a whole 2x2x4 slice. The times are simulated.
32 devices in a mesh: dp: 8 (over z, y), vocab: 4 (over x, core).
Axes of the slice: x: 2, y: 2, z: 4, core: 2. Of those that a mesh axis runs over, the one named last changes fastest.
Arguments:
- hidden_states: bfloat16 [4096, 2048], P('dp', 'vocab'), may hold values from -12 to 12
- teacher_logits: bfloat16 [4096, 16384], P('dp', 'vocab'), may hold values from -24 to 240
- head_weight: bfloat16 [2048, 16384], P(None, 'vocab'), as said below
Outputs:
- kl_per_token: float32 [4096], P('dp')
- hidden_grad: bfloat16 [4096, 2048], P('dp', 'vocab')
- head_grad: float32 [2048, 16384], P('dp', 'vocab')
Inputs may be any that keep to these rules, and one draw needn't show every extreme that they name: `head_weight`: every entry's magnitude is at most 18 / sqrt(2048).
All inputs are finite; a program needn't handle non-finite values.
Results may differ from a plain program's by a relative error of at most 0.014.
Values may be sent and summed in bfloat16 or wider, within the bound.
A program may use at most 128 MiB of HBM per device.

v0:
```python
import jax
import jax.numpy as jnp
from jax import lax
from jax.sharding import PartitionSpec as P

MICRO = 2


grad_scale = 8.0


def micro_batch(hidden_part, teacher_part, head_weight):
    gathered = lax.all_gather(hidden_part, "vocab", axis=1, tiled=True)
    student = jnp.dot(gathered, head_weight, preferred_element_type=jnp.float32)
    teacher = teacher_part.astype(jnp.float32)
    student_max, teacher_max = lax.pmax(
        (jnp.max(student, axis=1), jnp.max(teacher, axis=1)), "vocab"
    )
    student_terms = jnp.exp(student - student_max[:, None])
    teacher_terms = jnp.exp(teacher - teacher_max[:, None])
    student_total, teacher_total, cross_term = lax.psum(
        (
            jnp.sum(student_terms, axis=1),
            jnp.sum(teacher_terms, axis=1),
            jnp.sum(teacher_terms * (teacher - student), axis=1),
        ),
        "vocab",
    )
    divergence = (
        cross_term / teacher_total
        - teacher_max
        - jnp.log(teacher_total)
        + student_max
        + jnp.log(student_total)
    )
    logit_grad = (
        grad_scale
        * (student_terms / student_total[:, None] - teacher_terms / teacher_total[:, None])
    ).astype(jnp.bfloat16)
    partial_value = lax.dot_general(
        logit_grad, head_weight, (((1,), (1,)), ((), ())), preferred_element_type=jnp.float32
    )
    hidden_grad = lax.psum_scatter(
        partial_value.astype(jnp.bfloat16), "vocab", scatter_dimension=1, tiled=True
    )
    return (gathered, logit_grad, hidden_grad, divergence)


def per_device(hidden_states, teacher_logits, head_weight):
    device_rows = hidden_states.shape[0]
    micro_rows = device_rows // MICRO
    model_width = head_weight.shape[0]
    local_vocab = head_weight.shape[1]
    initial = jnp.zeros((model_width, local_vocab), jnp.float32)
    running = initial
    collected = []
    for number in range(MICRO):
        row_begin = number * micro_rows
        row_end = row_begin + micro_rows
        accumulate_running = running
        gathered, logit_grad, accumulate_hidden_grad, accumulate_divergence = micro_batch(
            hidden_states[row_begin:row_end], teacher_logits[row_begin:row_end], head_weight
        )
        accumulate_running = accumulate_running + lax.dot_general(
            gathered, logit_grad, (((0,), (0,)), ((), ())), preferred_element_type=jnp.float32
        )
        running = accumulate_running
        produced = (accumulate_hidden_grad, accumulate_divergence)
        collected.append(produced)
    results = tuple((jnp.concatenate(column, axis=0) for column in zip(*collected)))
    hidden_grad = results[0]
    divergence = results[1]
    head_grad = lax.psum_scatter(
        running.astype(jnp.bfloat16), "dp", scatter_dimension=0, tiled=True
    ).astype(jnp.float32)
    return (divergence, hidden_grad, head_grad)


def solution(mesh):
    in_specs = (P("dp", "vocab"), P("dp", "vocab"), P(None, "vocab"))
    out_specs = (P("dp"), P("dp", "vocab"), P("dp", "vocab"))
    return jax.shard_map(
        per_device, mesh=mesh, in_specs=in_specs, out_specs=out_specs, check_vma=False
    )
```

profile of v0, /device:TPU:0, one launch (start us, length us, event | category | flops | bytes accessed | tf_op | source)
XLA Modules:
  0.0 441.8 jit_solution(649472566438588968)
XLA Ops:
  7.2 0.0 all-gather.3.cloned.1.call-start
  7.2 1.9 fusion.24
  9.1 0.0 all-gather.3.cloned.1.call-update
  9.1 0.0 all-gather.5.cloned.1.call-start
  9.1 0.7 all-gather.5.cloned.1.call-update
  9.8 0.0 reduce-scatter.4.cloned.1.call-start
  9.9 2.9 slice_reduce_fusion.1
  12.7 16.8 %all-gather.3.cloned.1.call-done = bf16[256,2048]{1,0:T(8,128)(2,1)} async-done(((bf16[256,512]{1,0:T(8,128)(2,1)}), bf16[256,2048]{1,0:T(8,128)(2,1)}) %all-gather.3.cloned.1.call-update) | async-done | bytes 1048592 | tf_op jit(solution)/shard_map/all_gather | solution.py:13
  29.6 12.6 %fusion.26 = (f32[256]{0:T(256)S(1)}, f32[256,4096]{1,0:T(8,128)}) fusion(bf16[256,2048]{1,0:T(8,128)(2,1)} %all-gather.3.cloned.1.call-done, bf16[2048,4096]{1,0:T(8,128)(2,1)} %param.5), kind=kOutput, calls=%fused_computation.37 | convolution fusion | flops 4296015872 | bytes 22021120 | tf_op jit(solution)/shard_map/dot_general | solution.py:14
  42.2 6.2 %all-gather.5.cloned.1.call-done = bf16[256,2048]{1,0:T(8,128)(2,1)} async-done(((bf16[256,512]{1,0:T(8,128)(2,1)}), bf16[256,2048]{1,0:T(8,128)(2,1)}) %all-gather.5.cloned.1.call-update) | async-done | bytes 1048592 | tf_op jit(solution)/shard_map/all_gather | solution.py:13
  48.4 12.6 %fusion.25 = (f32[256]{0:T(256)S(1)}, f32[256,4096]{1,0:T(8,128)}) fusion(bf16[256,2048]{1,0:T(8,128)(2,1)} %all-gather.5.cloned.1.call-done, bf16[2048,4096]{1,0:T(8,128)(2,1)} %param.5), kind=kOutput, calls=%fused_computation.36 | convolution fusion | flops 4296015872 | bytes 22021120 | tf_op jit(solution)/shard_map/dot_general | solution.py:14
  61.1 5.9 %all-reduce.1 = (f32[256]{0:T(256)S(1)}, f32[256]{0:T(256)S(1)}, f32[256]{0:T(256)S(1)}, f32[256]{0:T(256)S(1)}) all-reduce(bf16[256]{0:T(256)(128)(2,1)S(1)} %get-tuple-element.14, bf16[256]{0:T(256)(128)(2,1)S(1)} %get-tuple-element.15, f32[256]{0:T(256)S(1)} %get-tuple-element.28, ...), channel_id=1, replica_groups=mesh['dp'=8,'vocab'=4] {'vocab'}, use_global_device_ids=true, to_apply=%region_1.0 | all-reduce | flops 1024 | bytes 7168 | tf_op jit(solution)/shard_map/pmax | solution.py:16
  66.9 7.0 %fusion.5 = (f32[256]{0:T(256)S(1)}, f32[256]{0:T(256)S(1)}, f32[256]{0:T(256)S(1)}, f32[256]{0:T(256)S(1)}, f32[256]{0:T(256)S(1)}, /*index=5*/f32[256]{0:T(256)S(1)}) fusion(f32[256,4096]{1,0:T(8,128)} %get-tuple-element.31, f32[256]{0:T(256)S(1)} %get-tuple-element.22, bf16[512,4096]{1,0:T(8,128)(2,1)} %param.4, f32[256]{0:T(256)S(1)} %get-tuple-element.23, ...), kind=kLoop, calls=%fused_computation.10 | loop fusion | flops 16775680 | bytes 12593152 | tf_op jit(solution)/shard_map/reduce_sum | solution.py:25
  73.9 5.9 %all-reduce = (f32[256]{0:T(256)S(1)}, f32[256]{0:T(256)S(1)}, f32[256]{0:T(256)S(1)}, f32[256]{0:T(256)S(1)}, f32[256]{0:T(256)S(1)}, /*index=5*/f32[256]{0:T(256)S(1)}) all-reduce(f32[256]{0:T(256)S(1)} %get-tuple-element.7, f32[256]{0:T(256)S(1)} %get-tuple-element.13, ...), channel_id=1, replica_groups=mesh['dp'=8,'vocab'=4] {'vocab'}, use_global_device_ids=true, to_apply=%region_5.0 | all-reduce | flops 1536 | bytes 12288 | tf_op jit(solution)/shard_map/psum | solution.py:21
  79.8 13.8 %convolution_convert_fusion.1 = bf16[256,2048]{1,0:T(8,128)(2,1)} fusion(bf16[2048,4096]{1,0:T(8,128)(2,1)} %param.5, f32[256,4096]{1,0:T(8,128)} %get-tuple-element.31, f32[256]{0:T(256)S(1)} %get-tuple-element.16, f32[256]{0:T(256)S(1)} %get-tuple-element.17, f32[256]{0:T(256)S(1)} %get-tuple-element.25, f32[256]{0:T(256)S(1)} %get-tuple-element.22, ...), kind=kOutput, calls=%fused_computation.27 | convolution fusion | flops 4303880192 | bytes 24121344 | tf_op jit(solution)/shard_map/dot_general | solution.py:40
  93.6 0.0 reduce-scatter.4.cloned.1.call-update
  93.6 0.0 reduce-scatter.6.cloned.1.call-start
  93.7 0.0 copy-start
  93.7 14.0 %convolution_convert_fusion = bf16[256,2048]{1,0:T(8,128)(2,1)} fusion(bf16[2048,4096]{1,0:T(8,128)(2,1)} %param.5, f32[256,4096]{1,0:T(8,128)} %get-tuple-element.29, f32[256]{0:T(256)S(1)} %get-tuple-element.18, f32[256]{0:T(256)S(1)} %get-tuple-element.19, f32[256]{0:T(256)S(1)} %get-tuple-element.24, f32[256]{0:T(256)S(1)} %get-tuple-element.23, ...), kind=kOutput, calls=%fused_computation.26 | convolution fusion | flops 4303880192 | bytes 24121344 | tf_op jit(solution)/shard_map/dot_general | solution.py:40
  107.7 0.0 reduce-scatter.6.cloned.1.call-update
  107.7 0.0 copy-start.1
  107.8 0.3 reduce-scatter.8.cloned.1.call-start
  108.0 0.0 copy-done
  108.0 17.0 %fusion.19 = f32[4096,2048]{1,0:T(8,128)} fusion(bf16[256,2048]{1,0:T(8,128)(2,1)S(1)} %copy-done, f32[256,4096]{1,0:T(8,128)} %get-tuple-element.31, f32[256]{0:T(256)S(1)} %get-tuple-element.16, f32[256]{0:T(256)S(1)} %get-tuple-element.17, f32[256]{0:T(256)S(1)} %get-tuple-element.25, f32[256]{0:T(256)S(1)} %get-tuple-element.22, bf16[512,4096]{1,0:T(8,128)(2,1)} %param.4), kind=kOutput, calls=%fused_computation.34 | convolution fusion | flops 4303355904 | bytes 40898560 | tf_op jit(solution)/shard_map/dot_general | solution.py:64
  125.0 0.0 copy-done.1
  125.0 21.8 %fusion = bf16[2048,4096]{0,1:T(8,128)(2,1)} fusion(f32[4096,2048]{1,0:T(8,128)} %fusion.19, bf16[256,2048]{1,0:T(8,128)(2,1)S(1)} %copy-done.1, f32[256,4096]{1,0:T(8,128)} %get-tuple-element.29, f32[256]{0:T(256)S(1)} %get-tuple-element.18, f32[256]{0:T(256)S(1)} %get-tuple-element.19, f32[256]{0:T(256)S(1)} %get-tuple-element.24, ...), kind=kOutput, calls=%fused_computation.1 | convolution fusion | flops 4320133120 | bytes 57675776 | tf_op jit(solution)/shard_map/dot_general | solution.py:64
  146.8 0.0 reduce-scatter.8.cloned.1.call-update
  146.9 0.6 pad_maximum_fusion.1
  147.5 0.0 reduce-scatter.4.cloned.1.call-done
  147.5 1.9 pad_maximum_fusion
  149.3 281.6 %reduce-scatter.8.cloned.1.call-done = bf16[256,4096]{0,1:T(8,128)(2,1)} async-done(((bf16[2048,4096]{0,1:T(8,128)(2,1)}), bf16[256,4096]{0,1:T(8,128)(2,1)}) %reduce-scatter.8.cloned.1.call-update) | async-done | bytes 2097168 | tf_op jit(solution)/shard_map/reduce_scatter | solution.py:73
  431.0 4.3 copy.6
  (2 shorter events, 0.0 us)
Async XLA Ops:
  7.2 22.4 %all-gather.3.cloned.1.call-start = ((), (), s32[]{:S(2)}) async-start(), calls=%async_computation.3 | async-start | bytes 1310720 | tf_op jit(solution)/shard_map/all_gather | solution.py:13
  9.1 39.3 %all-gather.5.cloned.1.call-start = ((), (), s32[]{:S(2)}) async-start(), calls=%async_computation.4 | async-start | bytes 1310720 | tf_op jit(solution)/shard_map/all_gather | solution.py:13
  9.8 137.6 %reduce-scatter.4.cloned.1.call-start = ((), (), s32[]{:S(2)}) async-start(), calls=%async_computation.5 | async-start | bytes 1310720 | tf_op jit(solution)/shard_map/reduce_scatter | solution.py:43
  93.6 53.8 %reduce-scatter.6.cloned.1.call-start = ((), (), s32[]{:S(2)}) async-start(), calls=%async_computation.6 | async-start | bytes 1310720 | tf_op jit(solution)/shard_map/reduce_scatter | solution.py:43
  93.7 14.3 %copy-start = (bf16[256,2048]{1,0:T(8,128)(2,1)S(1)}, bf16[256,2048]{1,0:T(8,128)(2,1)}, u32[]{:S(2)}) copy-start(bf16[256,2048]{1,0:T(8,128)(2,1)} %all-gather.3.cloned.1.call-done) | copy-start | bytes 3145732
  107.7 17.3 %copy-start.1 = (bf16[256,2048]{1,0:T(8,128)(2,1)S(1)}, bf16[256,2048]{1,0:T(8,128)(2,1)}, u32[]{:S(2)}) copy-start(bf16[256,2048]{1,0:T(8,128)(2,1)} %all-gather.5.cloned.1.call-done) | copy-start | bytes 3145732
  107.8 323.2 %reduce-scatter.8.cloned.1.call-start = ((), (), s32[]{:S(2)}) async-start(), calls=%async_computation.7 | async-start | bytes 18874368 | tf_op jit(solution)/shard_map/reduce_scatter | solution.py:73
Sparse Core Ops, SparseCore 0:
  10.1 19.4 all-gather.2
  31.7 16.6 all-gather.4
  93.8 26.1 reduce-scatter.3
  122.3 24.8 reduce-scatter.5
  150.8 280.0 reduce-scatter.7
where the time goes:
time: 442 us
  waiting for transfers between devices  305 us (69%)
  matrix products  91.9 us (21%)
  between operations  13.8 us (3%)
  other arithmetic  12.3 us (3%)
  blocking collectives  11.8 us (3%)
  local copies, waits for them, and re-layouts  6.14 us (1%)
    reduce_scatter x1, waiting for transfers between devices, per_device(): lax.psum_scatter(running.astype(jnp.bfloat16), 'dp', scatter_dimension=0,...  282 us
    dot_general x2, matrix products, per_device(): lax.dot_general(gathered, logit_grad, (((0,), (0,)), ((), ())), preferred...  38.8 us
    dot_general x2, matrix products, micro_batch(): lax.dot_general(logit_grad, head_weight, (((1,), (1,)), ((), ())), prefer...  27.8 us
    dot_general x2, matrix products, micro_batch(): student = jnp.dot(gathered, head_weight, preferred_element_type=jnp.float32)  25.3 us
    all_gather x2, waiting for transfers between devices, micro_batch(): gathered = lax.all_gather(hidden_part, 'vocab', axis=1, tiled=True)  23.1 us
  transfers between devices with their start and end apart: 5, of which 3 were waited for; matrix products, arithmetic and copies ran while one was open for 16% of the time, Pallas kernels for 0%

commit v1 on v0

v1 whole, which is shorter than its diff:
```python
import functools

import jax
import jax.numpy as jnp
from jax import lax
from jax.experimental import pallas as pl
from jax.experimental.pallas import tpu as pltpu
from jax.sharding import PartitionSpec as P

grad_scale = 8.0
PAIR = 2
MESH = pl.DeviceIdType.MESH


def slice_order(line):
    order = []
    low, high = 0, line - 1
    while low <= high:
        order.append(high)
        if low < high:
            order.append(low)
        low, high = low + 1, high - 1
    return order


def head_grad_kernel(
    line, chunks, width, rows, half,
    features_ref, grad_ref, out_ref,
    partner_grad, block, outgoing, incoming,
    pair_send, pair_recv, line_send, line_recv,
):
    me = lax.axis_index("dp")
    place = me // PAIR
    side = me - place * PAIR
    partner = place * PAIR + (PAIR - 1) - side
    has_down = place > 0
    has_up = place < line - 1
    up = jnp.where(has_up, me + PAIR, me)
    down = jnp.where(has_down, me - PAIR, me)

    barrier = pltpu.get_barrier_semaphore()
    pl.semaphore_signal(barrier, inc=1, device_id={"dp": partner}, device_id_type=MESH)

    @pl.when(has_down)
    def _():
        pl.semaphore_signal(barrier, inc=1, device_id={"dp": down}, device_id_type=MESH)

    @pl.when(has_up)
    def _():
        pl.semaphore_signal(barrier, inc=1, device_id={"dp": up}, device_id_type=MESH)

    pl.semaphore_wait(barrier, 1 + has_down.astype(jnp.int32) + has_up.astype(jnp.int32))

    def columns_of(chunk):
        return pl.ds(pl.multiple_of(chunk * width, width), width)

    def pair_copy(chunk):
        columns = columns_of(chunk)
        return pltpu.make_async_remote_copy(
            src_ref=grad_ref.at[:, columns],
            dst_ref=partner_grad.at[:, columns],
            send_sem=pair_send.at[chunk],
            recv_sem=pair_recv.at[chunk],
            device_id={"dp": partner},
            device_id_type=MESH,
        )

    def line_copy(chunk, part, slot, target):
        columns = columns_of(chunk)
        return pltpu.make_async_remote_copy(
            src_ref=outgoing.at[part, :, columns],
            dst_ref=incoming.at[slot, :, columns],
            send_sem=line_send.at[part, chunk],
            recv_sem=line_recv.at[slot, chunk],
            device_id={"dp": target},
            device_id_type=MESH,
        )

    @pl.loop(0, chunks)
    def _(chunk):
        pair_copy(chunk).start()

    def forward(chunk, part, has_source, slot, target):
        columns = columns_of(chunk)

        @pl.when(has_source)
        def _():
            line_copy(chunk, part, part, target).wait_recv()
            outgoing[part, :, columns] = (
                block[...] + incoming[part, :, columns].astype(jnp.float32)
            ).astype(jnp.bfloat16)

        @pl.when(jnp.logical_not(has_source))
        def _():
            outgoing[part, :, columns] = block[...].astype(jnp.bfloat16)

        line_copy(chunk, part, slot, target).start()

    def finish(chunk):
        columns = columns_of(chunk)

        @pl.when(has_down)
        def _():
            line_copy(chunk, 0, place, down).wait_recv()
            out_ref[:, columns] += incoming[place, :, columns].astype(jnp.float32)

        @pl.when(has_up)
        def _():
            line_copy(chunk, 0, line, up).wait_recv()
            out_ref[:, columns] += incoming[line, :, columns].astype(jnp.float32)

    lag = min(2, chunks)

    @pl.loop(0, chunks)
    def _(chunk):
        pair_copy(chunk).wait_recv()
        columns = columns_of(chunk)
        for part in slice_order(line):
            begin = part * rows
            block[...] = jnp.dot(
                features_ref[begin : begin + rows, :half],
                grad_ref[:, columns],
                preferred_element_type=jnp.float32,
            ) + jnp.dot(
                features_ref[begin : begin + rows, half:],
                partner_grad[:, columns],
                preferred_element_type=jnp.float32,
            )

            @pl.when(place == part)
            def _():
                out_ref[:, columns] = block[...]

            @pl.when(place < part)
            def _():
                forward(chunk, part, has_down, part, up)

            @pl.when(place > part)
            def _():
                forward(chunk, part, has_up, jnp.where(place - 1 == part, line, part), down)

        @pl.when(chunk >= lag)
        def _():
            finish(chunk - lag)

    @pl.loop(chunks - lag, chunks)
    def _(chunk):
        finish(chunk)

    @pl.loop(0, chunks)
    def _(chunk):
        pair_copy(chunk).wait_send()
        for part in range(line):

            @pl.when(place < part)
            def _():
                line_copy(chunk, part, part, up).wait_send()

            @pl.when(place > part)
            def _():
                line_copy(chunk, part, part, down).wait_send()


def reduce_head_grad(features, logit_grad, shards):
    line = shards // PAIR
    rows = features.shape[0] // line
    half, local_vocab = logit_grad.shape
    width = 256
    chunks = local_vocab // width
    return pl.pallas_call(
        functools.partial(head_grad_kernel, line, chunks, width, rows, half),
        out_shape=jax.ShapeDtypeStruct((rows, local_vocab), jnp.float32),
        in_specs=[pl.BlockSpec(memory_space=pltpu.VMEM)] * 2,
        out_specs=pl.BlockSpec(memory_space=pltpu.VMEM),
        scratch_shapes=[
            pltpu.VMEM((half, local_vocab), jnp.bfloat16),
            pltpu.VMEM((rows, width), jnp.float32),
            pltpu.VMEM((line, rows, local_vocab), jnp.bfloat16),
            pltpu.VMEM((line + 1, rows, local_vocab), jnp.bfloat16),
            pltpu.SemaphoreType.DMA((chunks,)),
            pltpu.SemaphoreType.DMA((chunks,)),
            pltpu.SemaphoreType.DMA((line, chunks)),
            pltpu.SemaphoreType.DMA((line + 1, chunks)),
        ],
        compiler_params=pltpu.CompilerParams(collective_id=0, has_side_effects=True),
    )(features, logit_grad)


def per_device(shards, hidden_states, teacher_logits, head_weight):
    tokens = hidden_states.shape[0]
    model_width = head_weight.shape[0]
    line = shards // PAIR
    rows = model_width // shards
    side = lax.axis_index("dp") % PAIR

    gathered = lax.all_gather(hidden_states, "vocab", axis=1, tiled=True)

    def slices(parity):
        return jnp.concatenate(
            [
                lax.dynamic_slice_in_dim(gathered, (part * PAIR + parity) * rows, rows, axis=1)
                for part in range(line)
            ],
            axis=1,
        )

    kept, given = slices(side), slices(1 - side)
    swap = [(index, index + 1 - 2 * (index % PAIR)) for index in range(shards)]
    received = lax.ppermute(given, "dp", swap)
    features = jnp.concatenate([kept.T, received.T], axis=1)

    student = jnp.dot(gathered, head_weight, preferred_element_type=jnp.float32)
    teacher = teacher_logits.astype(jnp.float32)
    student_top = jnp.max(student, axis=1)
    teacher_top = jnp.max(teacher, axis=1)
    teacher_terms = jnp.exp(teacher - teacher_top[:, None])
    stats = jnp.stack(
        [
            student_top,
            teacher_top,
            jnp.sum(jnp.exp(student - student_top[:, None]), axis=1),
            jnp.sum(teacher_terms, axis=1),
            jnp.sum(teacher_terms * (teacher - student), axis=1),
        ]
    )
    stats = lax.all_gather(stats, "vocab", axis=0, tiled=False)
    student_max = jnp.max(stats[:, 0], axis=0)
    teacher_max = jnp.max(stats[:, 1], axis=0)
    student_scale = jnp.exp(stats[:, 0] - student_max)
    teacher_scale = jnp.exp(stats[:, 1] - teacher_max)
    student_total = jnp.sum(stats[:, 2] * student_scale, axis=0)
    teacher_total = jnp.sum(stats[:, 3] * teacher_scale, axis=0)
    cross_term = jnp.sum(stats[:, 4] * teacher_scale, axis=0)
    student_log = student_max + jnp.log(student_total)
    teacher_log = teacher_max + jnp.log(teacher_total)
    divergence = cross_term / teacher_total - teacher_log + student_log
    logit_grad = (
        grad_scale
        * (jnp.exp(student - student_log[:, None]) - jnp.exp(teacher - teacher_log[:, None]))
    ).astype(jnp.bfloat16)
    logit_grad, features = lax.optimization_barrier((logit_grad, features))
    partial_value = lax.dot_general(
        logit_grad, head_weight, (((1,), (1,)), ((), ())), preferred_element_type=jnp.float32
    ).astype(jnp.bfloat16)
    partial_value, logit_grad = lax.optimization_barrier((partial_value, logit_grad))
    hidden_grad = lax.psum_scatter(partial_value, "vocab", scatter_dimension=1, tiled=True)
    head_grad = reduce_head_grad(features, logit_grad, shards)
    return (divergence, hidden_grad, head_grad)


def solution(mesh):
    in_specs = (P("dp", "vocab"), P("dp", "vocab"), P(None, "vocab"))
    out_specs = (P("dp"), P("dp", "vocab"), P("dp", "vocab"))
    return jax.shard_map(
        functools.partial(per_device, mesh.shape["dp"]),
        mesh=mesh, in_specs=in_specs, out_specs=out_specs, check_vma=False,
    )
```

time: 442 us -> 307 us (0.69)
  waiting for transfers between devices: 305 us -> 41.1 us
  Pallas kernels: 0 us -> 197 us
  matrix products: 91.9 us -> 26.2 us
  blocking collectives: 11.8 us -> 5.24 us
    reduce_scatter x3 -> x1, waiting for transfers between devices: 282 us -> 0.02 us  [per_device(): lax.psum_scatter(partial_value, 'vocab', scatter_dimension=1, tiled=True)]
    pallas_call x0 -> x1, Pallas kernels: none -> 197 us  [reduce_head_grad(): pl.pallas_call(functools.partial(head_grad_kernel, line, chunks, width, r...]
    dot_general x6 -> x2, matrix products: 91.9 us -> 26.2 us  [the longest x1 13.4 us: per_device(): lax.dot_general(logit_grad, head_weight, (((1,), (1,)), ((), ())), prefer...]
    ppermute x0 -> x1, waiting for transfers between devices: none -> 17.8 us  [per_device(): received = lax.ppermute(given, 'dp', swap)]
    psum x1 -> x0, blocking collectives: 5.93 us -> none  [micro_batch(): lax.psum((jnp.sum(student_terms, axis=1), jnp.sum(teacher_terms, axis=1),...]
    pmax x1 -> x0, blocking collectives: 5.85 us -> none  [micro_batch(): lax.pmax((jnp.max(student, axis=1), jnp.max(teacher, axis=1)), 'vocab')]
    convert_element_type x0 -> x1, other arithmetic: none -> 5.36 us  [per_device(): logit_grad = (grad_scale * (jnp.exp(student - student_log[:, None]) - jnp...]
    all_gather x0 -> x1, blocking collectives: none -> 5.24 us  [per_device(): stats = lax.all_gather(stats, 'vocab', axis=0, tiled=False)]
  transfers between devices with their start and end apart: 5 -> 3, of which waited for: 3 -> 2; matrix products, arithmetic and copies ran while one was open for 16% -> 3% of each run, Pallas kernels for 0% -> 64%
where the time goes in v1:
time: 307 us
  Pallas kernels  197 us (64%)
  waiting for transfers between devices  41.1 us (13%)
  matrix products  26.2 us (9%)
  other arithmetic  14.5 us (5%)
  between operations  14.2 us (5%)
  local copies, waits for them, and re-layouts  6.91 us (2%)
  blocking collectives  5.24 us (2%)
    pallas_call x1, Pallas kernels, reduce_head_grad(): pl.pallas_call(functools.partial(head_grad_kernel, line, chunks, width, r...  197 us
    all_gather x1, waiting for transfers between devices, per_device(): gathered = lax.all_gather(hidden_states, 'vocab', axis=1, tiled=True)  23.2 us
    ppermute x1, waiting for transfers between devices, per_device(): received = lax.ppermute(given, 'dp', swap)  17.8 us
    dot_general x1, matrix products, per_device(): lax.dot_general(logit_grad, head_weight, (((1,), (1,)), ((), ())), prefer...  13.4 us
    dot_general x1, matrix products, per_device(): student = jnp.dot(gathered, head_weight, preferred_element_type=jnp.float32)  12.8 us
    unnamed x12, local copies, waits for them, and re-layouts  6.73 us
  transfers between devices with their start and end apart: 3, of which 2 were waited for; matrix products, arithmetic and copies ran while one was open for 3% of the time, Pallas kernels for 64%

profile of v1, /device:TPU:0, one launch (start us, length us, event | category | flops | bytes accessed | tf_op | source)
XLA Modules:
  0.0 307.1 jit_solution(13241276649884433863)
XLA Ops:
  7.2 0.0 all-gather.4.cloned.1.call-start
  7.2 2.0 copy.10
  9.3 0.0 all-gather.4.cloned.1.call-update
  9.3 0.0 reduce-scatter.2.cloned.1.call-start
  9.4 2.8 reduce_max.46
  12.2 23.2 %all-gather.4.cloned.1.call-done = bf16[512,2048]{0,1:T(8,128)(2,1)} async-done(((bf16[512,512]{0,1:T(8,128)(2,1)}), bf16[512,2048]{0,1:T(8,128)(2,1)}) %all-gather.4.cloned.1.call-update) | async-done | bytes 2097168 | tf_op jit(solution)/shard_map/all_gather | solution.py:196
  35.4 0.0 copy-start
  35.4 12.8 %fusion.16 = (f32[512]{0:T(512)S(1)}, f32[512,4096]{1,0:T(8,128)S(1)}) fusion(bf16[512,2048]{0,1:T(8,128)(2,1)} %all-gather.4.cloned.1.call-done, bf16[2048,4096]{1,0:T(8,128)(2,1)} %param.5), kind=kOutput, calls=%fused_computation.42 | convolution fusion | flops 8592031744 | bytes 27265024 | tf_op jit(solution)/shard_map/dot_general | solution.py:212
  48.2 0.0 copy-start.2
  48.2 0.0 copy-done
  48.2 0.0 copy-start.4
  48.2 3.9 %fusion.3 = (f32[512]{0:T(512)S(1)}, f32[512]{0:T(512)S(1)}, f32[512]{0:T(512)S(1)}) fusion(bf16[512,4096]{1,0:T(8,128)(2,1)S(1)} %copy-done, f32[512,4096]{1,0:T(8,128)S(1)} %get-tuple-element.35, f32[512]{0:T(512)S(1)} %reduce_max.52, f32[512]{0:T(512)S(1)} %get-tuple-element.34), kind=kLoop, calls=%fused_computation.6 | loop fusion | flops 16775680 | bytes 12593152 | tf_op jit(solution)/shard_map/reduce_sum | solution.py:223
  52.1 0.0 copy-done.2
  52.2 5.2 %all-gather.1 = f32[4,5,512]{2,1,0:T(8,128)S(1)} all-gather(f32[1,5,512]{2,1,0:T(8,128)S(1)} %bitcast.46), channel_id=2, replica_groups=mesh['dp'=8,'vocab'=4] {'vocab'}, dimensions={0}, use_global_device_ids=true | all-gather | bytes 51200 | tf_op jit(solution)/shard_map/all_gather | solution.py:226
  57.5 0.0 copy-done.4
  57.5 0.0 copy-start.1
  57.5 0.2 constant_dynamic-slice_fusion.7
  57.6 0.1 pad_maximum_fusion.1
  57.7 1.5 collective-permute-start
  59.3 0.6 subtract_add_fusion
  59.9 0.1 maximum_bitcast_fusion
  60.0 0.0 copy-done.1
  60.0 5.4 %fusion.7.grad_ref = bf16[512,4096]{1,0:T(8,128)(2,1)S(1)} fusion(bf16[512,4096]{1,0:T(8,128)(2,1)S(1)} %copy-done.1, f32[512,4096]{1,0:T(8,128)} %copy-done.2, f32[512]{0:T(512)S(1)} %get-tuple-element.19, f32[512]{0:T(512)S(1)} %get-tuple-element.20), kind=kLoop, calls=%fused_computation.10 | loop fusion | flops 12582912 | bytes 16781312 | tf_op jit(solution)/shard_map/convert_element_type | solution.py:240
  65.3 0.0 copy-start.3
  65.4 17.8 %collective-permute-done = bf16[512,1024]{0,1:T(8,128)(2,1)S(1)} collective-permute-done((bf16[512,1024]{0,1:T(8,128)(2,1)S(1)}, bf16[512,1024]{0,1:T(8,128)(2,1)S(1)}, u32[]{:S(2)}, u32[]{:S(2)}) %collective-permute-start) | collective-permute-done | bytes 1048608 | tf_op jit(solution)/shard_map/ppermute | solution.py:209
  83.2 1.6 pad_maximum_fusion.features_ref
  84.8 0.0 copy-done.3
  84.8 13.4 %convolution_convert_fusion = bf16[512,2048]{1,0:T(8,128)(2,1)} fusion(bf16[512,4096]{1,0:T(8,128)(2,1)S(1)} %fusion.7.grad_ref, bf16[2048,4096]{1,0:T(8,128)(2,1)} %param.5), kind=kOutput, calls=%fused_computation.12 | convolution fusion | flops 8590983168 | bytes 23068672 | tf_op jit(solution)/shard_map/dot_general | solution.py:242
  98.3 0.0 reduce-scatter.2.cloned.1.call-update
  98.3 197.3 %shard_map.58 = f32[256,4096]{1,0:T(8,128)} custom-call(bf16[1024,1024]{1,0:T(8,128)(2,1)} %pad_maximum_fusion.features_ref, bf16[512,4096]{1,0:T(8,128)(2,1)} %copy-done.3), custom_call_target="tpu_custom_call" | custom-call | tf_op jit(solution)/shard_map/pallas_call | solution.py:170
  295.5 0.0 reduce-scatter.2.cloned.1.call-done
  295.6 4.7 %copy.42 = f32[256,4096]{1,0:T(8,128)} copy(f32[256,4096]{1,0:T(8,128)} %shard_map.58) | data formatting | bytes 8388608
  (4 shorter events, 0.1 us)
Async XLA Ops:
  7.2 28.3 %all-gather.4.cloned.1.call-start = ((), (), s32[]{:S(2)}) async-start(), calls=%async_computation.1 | async-start | bytes 2621440 | tf_op jit(solution)/shard_map/all_gather | solution.py:196
  9.3 286.3 %reduce-scatter.2.cloned.1.call-start = ((), (), s32[]{:S(2)}) async-start(), calls=%async_computation.2 | async-start | bytes 2621440 | tf_op jit(solution)/shard_map/reduce_scatter | solution.py:246
  35.4 12.8 %copy-start = (bf16[512,4096]{1,0:T(8,128)(2,1)S(1)}, bf16[512,4096]{1,0:T(8,128)(2,1)}, u32[]{:S(2)}) copy-start(bf16[512,4096]{1,0:T(8,128)(2,1)} %param.4) | copy-start | bytes 12582916
  48.2 3.9 %copy-start.2 = (f32[512,4096]{1,0:T(8,128)}, f32[512,4096]{1,0:T(8,128)S(1)}, u32[]{:S(2)}) copy-start(f32[512,4096]{1,0:T(8,128)S(1)} %get-tuple-element.35) | copy-start | bytes 25165828
  48.2 9.2 %copy-start.4 = (bf16[512,2048]{0,1:T(8,128)(2,1)S(1)}, bf16[512,2048]{0,1:T(8,128)(2,1)}, u32[]{:S(2)}) copy-start(bf16[512,2048]{0,1:T(8,128)(2,1)} %all-gather.4.cloned.1.call-done) | copy-start | bytes 6291460
  57.5 2.5 copy-start.1
  57.7 25.5 %collective-permute-start = (bf16[512,1024]{0,1:T(8,128)(2,1)S(1)}, bf16[512,1024]{0,1:T(8,128)(2,1)S(1)}, u32[]{:S(2)}, u32[]{:S(2)}) collective-permute-start(bf16[512,1024]{0,1:T(8,128)(2,1)S(1)} %pad_maximum_fusion.1), channel_id=1, source_target_pairs={{0,4},{4,0},{8,12},{12,8},{16,20},{20,16},{24,28},{28,24},{1,5},{5... | collective-permute-start | bytes 3145736 | tf_op jit(solution)/shard_map/ppermute | solution.py:209
  65.3 19.5 %copy-start.3 = (bf16[512,4096]{1,0:T(8,128)(2,1)}, bf16[512,4096]{1,0:T(8,128)(2,1)S(1)}, u32[]{:S(2)}) copy-start(bf16[512,4096]{1,0:T(8,128)(2,1)S(1)} %fusion.7.grad_ref) | copy-start | bytes 12582916
Sparse Core Ops, SparseCore 0:
  10.1 25.2 all-gather.3
  98.4 31.1 reduce-scatter.1

commit v2 on v1

--- a/solution.py
+++ b/solution.py
@@ -76,9 +76,23 @@
             device_id_type=MESH,
         )
 
-    @pl.loop(0, chunks)
+    ahead = min(3, chunks)
+    window = min(2, chunks)
+
+    @pl.loop(0, ahead)
     def _(chunk):
         pair_copy(chunk).start()
+
+    def drain(chunk):
+        for part in range(line):
+
+            @pl.when(place < part)
+            def _():
+                line_copy(chunk, part, part, up).wait_send()
+
+            @pl.when(place > part)
+            def _():
+                line_copy(chunk, part, part, down).wait_send()
 
     def forward(chunk, part, has_source, slot, target):
         columns = columns_of(chunk)
@@ -114,6 +128,15 @@
     @pl.loop(0, chunks)
     def _(chunk):
         pair_copy(chunk).wait_recv()
+
+        @pl.when(chunk + ahead < chunks)
+        def _():
+            pair_copy(chunk + ahead).start()
+
+        @pl.when(chunk >= window)
+        def _():
+            drain(chunk - window)
+
         columns = columns_of(chunk)
         for part in slice_order(line):
             begin = part * rows
@@ -147,18 +170,13 @@
     def _(chunk):
         finish(chunk)
 
+    @pl.loop(chunks - window, chunks)
+    def _(chunk):
+        drain(chunk)
+
     @pl.loop(0, chunks)
     def _(chunk):
         pair_copy(chunk).wait_send()
-        for part in range(line):
-
-            @pl.when(place < part)
-            def _():
-                line_copy(chunk, part, part, up).wait_send()
-
-            @pl.when(place > part)
-            def _():
-                line_copy(chunk, part, part, down).wait_send()
 
 
 def reduce_head_grad(features, logit_grad, shards):
@@ -207,7 +225,6 @@
     kept, given = slices(side), slices(1 - side)
     swap = [(index, index + 1 - 2 * (index % PAIR)) for index in range(shards)]
     received = lax.ppermute(given, "dp", swap)
-    features = jnp.concatenate([kept.T, received.T], axis=1)
 
     student = jnp.dot(gathered, head_weight, preferred_element_type=jnp.float32)
     teacher = teacher_logits.astype(jnp.float32)
@@ -223,7 +240,9 @@
             jnp.sum(teacher_terms * (teacher - student), axis=1),
         ]
     )
+    stats, received = lax.optimization_barrier((stats, received))
     stats = lax.all_gather(stats, "vocab", axis=0, tiled=False)
+    features = jnp.concatenate([kept.T, received.T], axis=1)
     student_max = jnp.max(stats[:, 0], axis=0)
     teacher_max = jnp.max(stats[:, 1], axis=0)
     student_scale = jnp.exp(stats[:, 0] - student_max)

time: 307 us -> 300 us (0.977)
  waiting for transfers between devices: 41.1 us -> 31.1 us
  local copies, waits for them, and re-layouts: 6.91 us -> 10.6 us
    ppermute x1, waiting for transfers between devices: 17.8 us -> 7.83 us  [per_device(): received = lax.ppermute(given, 'dp', swap)]
  transfers between devices with their start and end apart: 3 -> 3, of which waited for: 2 -> 2; matrix products, arithmetic and copies ran while one was open for 3% -> 6% of each run, Pallas kernels for 64% -> 66%
where the time goes in v2:
time: 300 us
  Pallas kernels  197 us (66%)
  waiting for transfers between devices  31.1 us (10%)
  matrix products  25.4 us (8%)
  other arithmetic  14.6 us (5%)
  between operations  14.2 us (5%)
  local copies, waits for them, and re-layouts  10.6 us (4%)
  blocking collectives  5.22 us (2%)
    pallas_call x1, Pallas kernels, reduce_head_grad(): pl.pallas_call(functools.partial(head_grad_kernel, line, chunks, width, r...  197 us
    all_gather x1, waiting for transfers between devices, per_device(): gathered = lax.all_gather(hidden_states, 'vocab', axis=1, tiled=True)  23.2 us
    dot_general x1, matrix products, per_device(): lax.dot_general(logit_grad, head_weight, (((1,), (1,)), ((), ())), prefer...  13.4 us
    dot_general x1, matrix products, per_device(): student = jnp.dot(gathered, head_weight, preferred_element_type=jnp.float32)  11.9 us
    unnamed x12, local copies, waits for them, and re-layouts  8.73 us
    ppermute x1, waiting for transfers between devices, per_device(): received = lax.ppermute(given, 'dp', swap)  7.83 us
  transfers between devices with their start and end apart: 3, of which 2 were waited for; matrix products, arithmetic and copies ran while one was open for 6% of the time, Pallas kernels for 66%

profile of v2, /device:TPU:0, one launch (start us, length us, event | category | flops | bytes accessed | tf_op | source)
XLA Modules:
  0.0 300.2 jit_solution(12785606905717433119)
XLA Ops:
  7.2 0.0 all-gather.4.cloned.1.call-start
  7.2 2.0 copy.10
  9.3 0.0 all-gather.4.cloned.1.call-update
  9.3 0.0 reduce-scatter.2.cloned.1.call-start
  9.4 2.8 reduce_max.46
  12.2 23.2 %all-gather.4.cloned.1.call-done = bf16[512,2048]{0,1:T(8,128)(2,1)} async-done(((bf16[512,512]{0,1:T(8,128)(2,1)}), bf16[512,2048]{0,1:T(8,128)(2,1)}) %all-gather.4.cloned.1.call-update) | async-done | bytes 2097168 | tf_op jit(solution)/shard_map/all_gather | solution.py:214
  35.4 0.0 copy-start.4
  35.4 1.9 constant_dynamic-slice_fusion.3
  37.3 0.1 pad_maximum_fusion.1
  37.4 0.0 copy-start
  37.4 1.5 collective-permute-start
  38.9 0.0 copy-done.4
  38.9 11.9 %fusion.16 = (f32[512]{0:T(512)S(1)}, f32[512,4096]{1,0:T(8,128)S(1)}) fusion(bf16[512,2048]{0,1:T(8,128)(2,1)S(1)} %copy-done.4, bf16[2048,4096]{1,0:T(8,128)(2,1)} %param.5), kind=kOutput, calls=%fused_computation.42 | convolution fusion | flops 8592031744 | bytes 27265024 | tf_op jit(solution)/shard_map/dot_general | solution.py:229
  50.9 0.0 copy-start.2
  50.9 0.0 copy-done
  50.9 3.9 %fusion.3 = (f32[512]{0:T(512)S(1)}, f32[512]{0:T(512)S(1)}, f32[512]{0:T(512)S(1)}) fusion(bf16[512,4096]{1,0:T(8,128)(2,1)S(1)} %copy-done, f32[512,4096]{1,0:T(8,128)S(1)} %get-tuple-element.39, f32[512]{0:T(512)S(1)} %reduce_max.52, f32[512]{0:T(512)S(1)} %get-tuple-element.38), kind=kLoop, calls=%fused_computation.6 | loop fusion | flops 16775680 | bytes 12593152 | tf_op jit(solution)/shard_map/reduce_sum | solution.py:240
  54.8 0.0 copy-done.2
  54.8 0.0 copy-start.1
  54.8 0.1 maximum_bitcast_fusion
  54.9 7.8 %collective-permute-done = bf16[512,1024]{0,1:T(8,128)(2,1)S(1)} collective-permute-done((bf16[512,1024]{0,1:T(8,128)(2,1)S(1)}, bf16[512,1024]{0,1:T(8,128)(2,1)S(1)}, u32[]{:S(2)}, u32[]{:S(2)}) %collective-permute-start) | collective-permute-done | bytes 1048608 | tf_op jit(solution)/shard_map/ppermute | solution.py:227
  62.8 5.2 %all-gather.1 = f32[4,5,512]{2,1,0:T(8,128)S(1)} all-gather(f32[1,5,512]{2,1,0:T(8,128)S(1)} %bitcast.46), channel_id=2, replica_groups=mesh['dp'=8,'vocab'=4] {'vocab'}, dimensions={0}, use_global_device_ids=true | all-gather | bytes 51200 | tf_op jit(solution)/shard_map/all_gather | solution.py:244
  68.0 1.7 pad_maximum_fusion.features_ref
  69.7 0.6 subtract_add_fusion
  70.3 0.0 copy-done.1
  70.3 5.4 %fusion.7.grad_ref = bf16[512,4096]{1,0:T(8,128)(2,1)S(1)} fusion(bf16[512,4096]{1,0:T(8,128)(2,1)S(1)} %copy-done.1, f32[512,4096]{1,0:T(8,128)} %copy-done.2, f32[512]{0:T(512)S(1)} %get-tuple-element.23, f32[512]{0:T(512)S(1)} %get-tuple-element.24), kind=kLoop, calls=%fused_computation.10 | loop fusion | flops 12582912 | bytes 16781312 | tf_op jit(solution)/shard_map/convert_element_type | solution.py:259
  75.7 0.0 copy-start.3
  75.7 2.0 copy-done.3
  77.7 13.4 %convolution_convert_fusion = bf16[512,2048]{1,0:T(8,128)(2,1)} fusion(bf16[512,4096]{1,0:T(8,128)(2,1)S(1)} %fusion.7.grad_ref, bf16[2048,4096]{1,0:T(8,128)(2,1)} %param.5), kind=kOutput, calls=%fused_computation.12 | convolution fusion | flops 8590983168 | bytes 23068672 | tf_op jit(solution)/shard_map/dot_general | solution.py:261
  91.2 0.0 reduce-scatter.2.cloned.1.call-update
  91.2 197.5 %shard_map.58 = f32[256,4096]{1,0:T(8,128)} custom-call(bf16[1024,1024]{1,0:T(8,128)(2,1)} %pad_maximum_fusion.features_ref, bf16[512,4096]{1,0:T(8,128)(2,1)} %copy-done.3), custom_call_target="tpu_custom_call" | custom-call | tf_op jit(solution)/shard_map/pallas_call | solution.py:188
  288.7 0.0 reduce-scatter.2.cloned.1.call-done
  288.7 4.7 %copy.42 = f32[256,4096]{1,0:T(8,128)} copy(f32[256,4096]{1,0:T(8,128)} %shard_map.58) | data formatting | bytes 8388608
  (4 shorter events, 0.1 us)
Async XLA Ops:
  7.2 28.3 %all-gather.4.cloned.1.call-start = ((), (), s32[]{:S(2)}) async-start(), calls=%async_computation.1 | async-start | bytes 2621440 | tf_op jit(solution)/shard_map/all_gather | solution.py:214
  9.3 279.4 %reduce-scatter.2.cloned.1.call-start = ((), (), s32[]{:S(2)}) async-start(), calls=%async_computation.2 | async-start | bytes 2621440 | tf_op jit(solution)/shard_map/reduce_scatter | solution.py:265
  35.4 3.5 %copy-start.4 = (bf16[512,2048]{0,1:T(8,128)(2,1)S(1)}, bf16[512,2048]{0,1:T(8,128)(2,1)}, u32[]{:S(2)}) copy-start(bf16[512,2048]{0,1:T(8,128)(2,1)} %all-gather.4.cloned.1.call-done) | copy-start | bytes 6291460
  37.4 13.5 %copy-start = (bf16[512,4096]{1,0:T(8,128)(2,1)S(1)}, bf16[512,4096]{1,0:T(8,128)(2,1)}, u32[]{:S(2)}) copy-start(bf16[512,4096]{1,0:T(8,128)(2,1)} %param.4) | copy-start | bytes 12582916
  37.4 25.4 %collective-permute-start = (bf16[512,1024]{0,1:T(8,128)(2,1)S(1)}, bf16[512,1024]{0,1:T(8,128)(2,1)S(1)}, u32[]{:S(2)}, u32[]{:S(2)}) collective-permute-start(bf16[512,1024]{0,1:T(8,128)(2,1)S(1)} %pad_maximum_fusion.1), channel_id=1, source_target_pairs={{0,4},{4,0},{8,12},{12,8},{16,20},{20,16},{24,28},{28,24},{1,5},{5... | collective-permute-start | bytes 3145736 | tf_op jit(solution)/shard_map/ppermute | solution.py:227
  50.9 3.9 %copy-start.2 = (f32[512,4096]{1,0:T(8,128)}, f32[512,4096]{1,0:T(8,128)S(1)}, u32[]{:S(2)}) copy-start(f32[512,4096]{1,0:T(8,128)S(1)} %get-tuple-element.39) | copy-start | bytes 25165828
  54.8 15.5 %copy-start.1 = (bf16[512,4096]{1,0:T(8,128)(2,1)S(1)}, bf16[512,4096]{1,0:T(8,128)(2,1)}, u32[]{:S(2)}) copy-start(bf16[512,4096]{1,0:T(8,128)(2,1)} %param.4) | copy-start | bytes 12582916
  75.7 2.0 copy-start.3
Sparse Core Ops, SparseCore 0:
  10.1 25.2 all-gather.3
  91.3 31.1 reduce-scatter.1
